TPU v7x, 32 devices: a whole 2x2x4 slice. The times are simulated.
32 devices in a mesh: seq: 8 (over y, x, core), exp: 4 (over z).
Axes of the slice: x: 2, y: 2, z: 4, core: 2. Of those that a mesh axis runs over, the one named last changes fastest.
Arguments:
- grad_out: bfloat16 [4096, 2048], P(('seq', 'exp')), may hold values from -6 to 6
- out_proj: bfloat16 [4096, 2048], P('exp'), may hold values from -0.125 to 0.125
- step_size: float32 [64, 4096], P('exp', 'seq'), may hold values from 0.001 to 0.1
- log_decay: float32 [64, 4096], P('exp', 'seq'), may hold values from -1 to 0, as said below
- b_input: float32 [16, 4096], P(None, 'seq'), may hold values from -1.5 to 1.5
- c_output: float32 [16, 4096], P(None, 'seq'), may hold values from -1.5 to 1.5
- skip_gain: float32 [4096], P('exp'), may hold values from 0.5 to 1.5
- expert_ids: int32 [4096, 2], P('seq'), may hold values from 0 to 3, all different within a row; in each aligned block of 128 rows (0 to 127, 128 to 255, ...) at most 66 rows name the same one
- hidden_act: bfloat16 [4, 32, 66, 8192], P('exp', None, None, 'seq'), may hold values from -6 to 6
- w_down: bfloat16 [4, 8192, 2048], P('exp', 'seq'), may hold values from -0.0029296875 to 0.0029296875
Outputs:
- d_inner: bfloat16 [4096, 4096], P('seq', 'exp')
- d_gate: float32 [2, 4096], P(None, ('seq', 'exp'))
Inputs may be any that keep to these rules, and one draw needn't show every extreme that they name: `expert_ids`: each row names 2 different experts. Within the rows of one token group no expert is named by more than 66 rows, and in every draw some expert is named by exactly 66 rows of some group. `log_decay`: every entry is negative.
All inputs are finite; a program needn't handle non-finite values.
Results may differ from a plain program's by a relative error of at most 0.00065.
Values may be sent and summed in bfloat16 or wider, within the bound.
No kernel may reach another device: no remote copies, remote signals or barrier semaphores. Data moves between devices by JAX's collectives and lax.ppermute only.
A program may use at most 128 MiB of HBM per device.

v0:
```python
import jax
import jax.numpy as jnp
from jax import lax
from jax.sharding import PartitionSpec as P

HEAD = 64
highest = lax.Precision.HIGHEST


def block_pass(state_in, pieces):
    grad_block, decay_block, step_block, b_block, c_block = pieces
    cum_decay = jnp.cumsum(decay_block, axis=1)
    gap_table = cum_decay[:, None, :] - cum_decay[:, :, None]
    upper_mask = lax.broadcasted_iota(jnp.int32, gap_table.shape, 2) >= lax.broadcasted_iota(
        jnp.int32, gap_table.shape, 1
    )
    weights = jnp.where(upper_mask, jnp.exp(jnp.where(upper_mask, gap_table, 0.0)), 0.0)
    intersection = lax.dot_general(
        b_block,
        c_block,
        (((0,), (0,)), ((), ())),
        precision=highest,
        preferred_element_type=jnp.float32,
    )
    within = jnp.einsum("hut,thp->uhp", weights * intersection[None], grad_block, precision=highest)
    tail_decay = jnp.exp(cum_decay[:, -1:] - cum_decay)
    from_state = (
        jnp.einsum("nu,hnp->uhp", b_block, state_in, precision=highest) * tail_decay.T[:, :, None]
    )
    result = step_block.T[:, :, None] * (within + from_state)
    state_out = jnp.einsum(
        "ht,nt,thp->hnp", jnp.exp(cum_decay), c_block, grad_block, precision=highest
    )
    state_out = state_out + jnp.exp(cum_decay[:, -1])[:, None, None] * state_in
    return (state_out, result)


def local_sweep(grad_rows, decay_rows, step_rows, b_rows, c_rows, start_state):
    row_count = grad_rows.shape[0]
    head_count = decay_rows.shape[0]
    block_len = min(512, row_count)
    block_count = row_count // block_len
    pieces = (
        grad_rows.reshape(block_count, block_len, head_count, grad_rows.shape[2]),
        decay_rows.reshape(head_count, block_count, block_len).transpose(1, 0, 2),
        step_rows.reshape(head_count, block_count, block_len).transpose(1, 0, 2),
        b_rows.reshape(b_rows.shape[0], block_count, block_len).transpose(1, 0, 2),
        c_rows.reshape(c_rows.shape[0], block_count, block_len).transpose(1, 0, 2),
    )
    state_out, results = lax.scan(block_pass, start_state, pieces, reverse=True)
    return (state_out, results.reshape(row_count, head_count, grad_rows.shape[2]))


def route_table(groups, expert, cap_len):
    hit_mask = jnp.any(groups == expert, axis=2)
    rank_ids = jnp.cumsum(hit_mask.astype(jnp.int32), axis=1) - 1
    slot_ids = lax.broadcasted_iota(jnp.int32, (1, 1, cap_len), 2)
    chosen = jnp.logical_and(hit_mask[:, :, None], rank_ids[:, :, None] == slot_ids)
    token_ids = lax.broadcasted_iota(jnp.int32, chosen.shape, 1)
    position = jnp.sum(jnp.where(chosen, token_ids, 0), axis=1)
    filled = jnp.any(chosen, axis=1)
    return (position, filled)


def slot_lookup(slot_table, own_ids, cap_len, expert_count):
    experts_iota = lax.broadcasted_iota(jnp.int32, (1, 1, expert_count), 2)
    onehot = own_ids[:, :, None] == experts_iota
    member = jnp.any(onehot, axis=1).astype(jnp.int32)
    rank_ids = jnp.cumsum(member, axis=0) - 1
    slot_of = jnp.sum(jnp.where(onehot, rank_ids[:, None, :], 0), axis=2)
    picked = jnp.sum(jnp.where(onehot[:, :, :, None], slot_table[None, None], 0.0), axis=2)
    slot_iota = lax.broadcasted_iota(jnp.int32, (1, 1, cap_len), 2)
    return jnp.sum(jnp.where(slot_of[:, :, None] == slot_iota, picked, 0.0), axis=2)


def shards(
    grad_out,
    out_proj,
    step_size,
    log_decay,
    b_input,
    c_output,
    skip_gain,
    expert_ids,
    hidden_act,
    w_down,
):
    exp_index = lax.axis_index("exp")
    seq_index = lax.axis_index("seq")
    exp_count = lax.axis_size("exp")
    seq_count = lax.axis_size("seq")
    tok_len = grad_out.shape[0]
    cap_len = hidden_act.shape[2]
    gathered = lax.all_gather(grad_out, "exp", axis=0, tiled=True)
    groups = expert_ids.reshape(exp_count, tok_len, expert_ids.shape[1])
    position, filled = route_table(groups, exp_index, cap_len)
    flat_index = (position + lax.broadcasted_iota(jnp.int32, position.shape, 0) * tok_len).reshape(
        -1
    )
    slot_rows = jnp.take(gathered, flat_index, axis=0)
    slot_rows = jnp.where(filled.reshape(-1, 1), slot_rows, jnp.zeros_like(slot_rows))
    saved_rows = hidden_act.reshape(-1, hidden_act.shape[3])
    weights = w_down[0]
    projected = lax.dot_general(
        lax.all_gather(slot_rows, "seq", axis=0, tiled=True),
        weights,
        (((1,), (1,)), ((), ())),
        preferred_element_type=jnp.float32,
    )
    partial_scores = jnp.sum(projected * saved_rows.astype(jnp.float32), axis=1)
    head_count = out_proj.shape[0] // HEAD
    inner_grad = lax.dot_general(
        gathered, out_proj, (((1,), (1,)), ((), ())), preferred_element_type=jnp.float32
    )
    row_count = inner_grad.shape[0]
    start_state = jnp.zeros((head_count, b_input.shape[0], HEAD), jnp.float32)
    summary, swept_part = local_sweep(
        inner_grad.reshape(row_count, head_count, HEAD),
        log_decay,
        step_size,
        b_input,
        c_output,
        start_state,
    )
    total_decay = jnp.sum(log_decay, axis=1)
    all_states, all_decay = (
        lax.all_gather(summary[None], "seq", axis=0, tiled=True),
        lax.all_gather(total_decay[None], "seq", axis=0, tiled=True),
    )
    shard_ids = lax.broadcasted_iota(jnp.int32, all_decay.shape, 0)
    beyond = jnp.where(shard_ids > seq_index, all_decay, 0.0)
    exponent = jnp.cumsum(beyond, axis=0) - beyond
    factor = jnp.where(
        shard_ids > seq_index, jnp.exp(jnp.where(shard_ids > seq_index, exponent, 0.0)), 0.0
    )
    incoming = jnp.sum(factor[:, :, None, None] * all_states, axis=0)
    suffix = jnp.flip(jnp.cumsum(jnp.flip(log_decay, 1), axis=1), 1) - log_decay
    from_carry = (
        jnp.einsum("nu,hnp->uhp", b_input, incoming, precision=highest)
        * jnp.exp(suffix).T[:, :, None]
    )
    combined = swept_part + step_size.T[:, :, None] * from_carry
    d_inner = (combined.reshape(row_count, -1) + skip_gain * inner_grad).astype(jnp.bfloat16)
    summed = lax.psum_scatter(
        partial_scores.reshape(seq_count, exp_count, cap_len),
        "seq",
        scatter_dimension=0,
        tiled=True,
    )
    slot_table = lax.all_to_all(
        summed.reshape(exp_count, 1, cap_len), "exp", split_axis=0, concat_axis=1, tiled=True
    ).reshape(exp_count, cap_len)
    own_ids = lax.dynamic_slice_in_dim(expert_ids, exp_index * tok_len, tok_len, 0)
    d_gate = slot_lookup(slot_table, own_ids, cap_len, exp_count).T
    return (d_inner, d_gate)


def solution(mesh):
    in_specs = (
        P(("seq", "exp"), None),
        P("exp", None),
        P("exp", "seq"),
        P("exp", "seq"),
        P(None, "seq"),
        P(None, "seq"),
        P("exp"),
        P("seq", None),
        P("exp", None, None, "seq"),
        P("exp", "seq", None),
    )
    out_specs = (P("seq", "exp"), P(None, ("seq", "exp")))
    return jax.shard_map(shards, mesh=mesh, in_specs=in_specs, out_specs=out_specs, check_vma=False)
```

profile of v0, /device:TPU:0, one launch (start us, length us, event | category | flops | bytes accessed | tf_op | source)
XLA Modules:
  0.0 207.7 jit_solution(10610763480653563069)
XLA Ops:
  7.2 0.7 all-gather.5.cloned.1.call-update
  8.0 0.7 compare_reduce_fusion
  8.7 0.3 reduce_window_sum.73
  9.0 1.2 select_reduce_fusion.1
  10.5 1.2 fusion.21
  12.0 46.0 %all-gather.5.cloned.1.call-done = bf16[512,2048]{1,0:T(8,128)(2,1)} async-done(((bf16[128,2048]{1,0:T(8,128)(2,1)}), bf16[512,2048]{1,0:T(8,128)(2,1)}) %all-gather.5.cloned.1.call-update) | async-done | bytes 2097168 | tf_op jit(solution)/shard_map/all_gather | solution.py:94
  58.0 6.2 %gather_fusion = bf16[264,2048]{1,0:T(8,128)(2,1)S(1)} fusion(bf16[512,2048]{1,0:T(8,128)(2,1)} %all-gather.5.cloned.1.call-done, s32[1024]{0:T(1024)S(1)} %pad_clamp_fusion), kind=kCustom, calls=%fused_computation | custom fusion | bytes 2163744 | tf_op jit(solution)/shard_map/jit(_take)/gather | solution.py:100
  64.2 1.2 select_select_fusion
  65.5 0.3 rev.7
  65.8 1.1 reduce-window.14
  67.1 1.2 reduce-window.16
  68.9 8.6 %copy.85 = f32[1,32,66,1024]{3,2,1,0:T(8,128)} copy(bf16[1,32,66,1024]{3,1,2,0:T(8,128)(2,1)} %param.18) | data formatting | bytes 12976128 | tf_op jit(solution)/shard_map/convert_element_type | solution.py:110
  77.5 9.5 %reshape.166 = f32[2112,1024]{1,0:T(8,128)} reshape(f32[1,32,66,1024]{3,2,1,0:T(8,128)} %copy.85) | data formatting | bytes 17301504 | tf_op jit(solution)/shard_map/convert_element_type | solution.py:110
  87.0 0.8 constant_dynamic-slice_fusion.1
  88.2 0.6 fusion.31
  90.2 2.0 fusion.33
  92.2 3.1 %fusion.22 = f32[16,64,512]{2,1,0:T(8,128)} fusion(f32[16,512]{1,0:T(8,128)S(1)} %copy-done), kind=kOutput, calls=%fused_computation.34 | convolution fusion | flops 100663296 | bytes 2129920 | tf_op jit(solution)/shard_map/while/body/eval_jaxpr/nu,hnp->uhp/dot_general | solution.py:28
  95.3 5.9 %fusion.32 = f32[512,1024]{1,0:T(8,128)} fusion(bf16[512,2048]{1,0:T(8,128)(2,1)S(1)} %copy-done.1, bf16[1024,2048]{1,0:T(8,128)(2,1)} %param.11), kind=kOutput, calls=%fused_computation.74 | convolution fusion | flops 2147483648 | bytes 8388608 | tf_op jit(solution)/shard_map/dot_general | solution.py:112
  101.2 2.1 %copy.75 = f32[512,1024]{0,1:T(8,128)S(1)} copy(f32[512,1024]{1,0:T(8,128)} %fusion.32) | data formatting | bytes 4194304 | tf_op jit(solution)/shard_map/dot_general | solution.py:112
  103.3 1.8 convolution_add_fusion
  105.1 16.7 %all-gather.1 = f32[128,16,64]{2,1,0:T(8,128)S(1)} all-gather(f32[16,16,64]{2,1,0:T(8,128)S(1)} %convolution_add_fusion), channel_id=3, replica_groups=mesh['seq'=8,'exp'=4] {'seq'}, dimensions={0}, use_global_device_ids=true | all-gather | bytes 589824 | tf_op jit(solution)/shard_map/all_gather | solution.py:127
  121.7 2.2 %all-gather.7.cloned.1.call-done = bf16[2112,2048]{1,0:T(8,128)(2,1)} async-done(((bf16[264,2048]{1,0:T(8,128)(2,1)}), bf16[2112,2048]{1,0:T(8,128)(2,1)}) %all-gather.7.cloned.1.call-update) | async-done | bytes 8650768 | tf_op jit(solution)/shard_map/all_gather | solution.py:105
  123.9 14.9 %multiply_reduce_fusion = f32[2112]{0:T(1024)S(1)} fusion(f32[2112,1024]{1,0:T(8,128)} %reshape.166, bf16[2112,2048]{1,0:T(8,128)(2,1)} %all-gather.7.cloned.1.call-done, bf16[1,1024,2048]{2,1,0:T(8,128)(2,1)} %param.19), kind=kOutput, calls=%fused_computation.8 | convolution fusion | flops 8862693376 | bytes 21504256 | tf_op jit(solution)/shard_map/dot_general | solution.py:104
  139.0 23.5 %all-reduce.2 = (f32[128]{0:T(128)S(1)}, f32[8,4,66]{2,1,0:T(4,128)S(1)}) all-reduce(f32[128]{0:T(128)S(1)} %dynamic-update-slice, f32[8,4,66]{2,1,0:T(4,128)S(1)} %reshape.164), channel_id=2, replica_groups=mesh['seq'=8,'exp'=4] {'seq'}, use_global_device_ids=true, to_apply=%add | all-reduce | flops 2240 | bytes 17920
  163.0 1.8 fusion.24
  164.8 20.5 %fusion.12 = f32[512,16,64]{0,2,1:T(8,128)} fusion(f32[16,64,512]{2,1,0:T(8,128)S(1)} %fusion.24, f32[16,64,512]{2,1,0:T(8,128)S(1)} %copy-done.3, f32[512,16,64]{0,2,1:T(8,128)S(1)} %bitcast.79, f32[512,512]{1,0:T(8,128)S(1)} %copy-done.4, f32[16,512]{1,0:T(8,128)S(1)} %copy_bitcast_fusion.1, f32[512,16]{0,1:T(8,128)S(1)} %get-tuple-element.22, ...), kind=kOutput, calls=%fused_computation.16 | convolution fusion | flops 3244818432 | bytes 9568256 | tf_op jit(solution)/shard_map/while/body/eval_jaxpr/hut,thp->uhp/dot_general | solution.py:25
  185.4 3.0 %copy.80 = f32[512,1024]{1,0:T(8,128)} copy(f32[512,1024]{0,1:T(8,128)} %bitcast.81) | data formatting | bytes 4194304 | tf_op jit(solution)/shard_map/reshape | solution.py:143
  188.4 1.2 constant_dynamic-slice_fusion
  189.6 4.7 %all-to-all-start = ((f32[4,1,66]{2,1,0:T(1,128)}), f32[4,1,66]{2,1,0:T(1,128)S(1)}, u32[]{:S(2)}, u32[]{:S(2)}) async-start(f32[4,1,66]{2,1,0:T(1,128)} %bitcast.17), calls=%async_computation | async-start | bytes 4096 | tf_op jit(solution)/shard_map/all_to_all | solution.py:150
  194.3 3.1 %add_convert_fusion = bf16[512,1024]{1,0:T(8,128)(2,1)} fusion(f32[512,1024]{1,0:T(8,128)} %copy.80, f32[512,1024]{1,0:T(8,128)S(1)} %copy-done.2, f32[1024]{0:T(1024)S(1)} %copy-done.7), kind=kLoop, calls=%fused_computation.19 | loop fusion | flops 1572864 | bytes 5246976 | tf_op jit(solution)/shard_map/convert_element_type | solution.py:143
  197.4 2.5 %all-to-all-done = f32[4,1,66]{2,1,0:T(1,128)S(1)} async-done(((f32[4,1,66]{2,1,0:T(1,128)}), f32[4,1,66]{2,1,0:T(1,128)S(1)}, u32[]{:S(2)}, u32[]{:S(2)}) %all-to-all-start) | async-done | bytes 1088 | tf_op jit(solution)/shard_map/all_to_all | solution.py:150
  200.2 0.6 select_reduce_fusion.2
  (68 shorter events, 3.5 us)
Async XLA Ops:
  7.2 83.1 %copy-start = (f32[16,512]{1,0:T(8,128)S(1)}, f32[16,512]{1,0:T(8,128)}, u32[]{:S(2)}) copy-start(f32[16,512]{1,0:T(8,128)} %param.14) | copy-start | bytes 98308
  7.2 50.8 %all-gather.5.cloned.1.call-start = ((), (), s32[]{:S(2)}) async-start(), calls=%async_computation.1 | async-start | bytes 2621440 | tf_op jit(solution)/shard_map/all_gather | solution.py:94
  7.9 116.0 %all-gather.7.cloned.1.call-start = ((), (), s32[]{:S(2)}) async-start(), calls=%async_computation.2 | async-start | bytes 9732096 | tf_op jit(solution)/shard_map/all_gather | solution.py:105
  64.2 1.3 copy-start.5
  77.5 10.7 %copy-start.8 = (u32[32]{0:T(128)S(1)}, u32[32]{0:T(128)}, u32[]{:S(2)}) copy-start(u32[32]{0:T(128)} %constant.76) | copy-start | bytes 388
  77.5 12.8 %copy-start.6 = (f32[16,512]{1,0:T(8,128)S(1)}, f32[16,512]{1,0:T(8,128)}, u32[]{:S(2)}) copy-start(f32[16,512]{1,0:T(8,128)} %param.15) | copy-start | bytes 98308
  87.0 8.3 %copy-start.1 = (bf16[512,2048]{1,0:T(8,128)(2,1)S(1)}, bf16[512,2048]{1,0:T(8,128)(2,1)}, u32[]{:S(2)}) copy-start(bf16[512,2048]{1,0:T(8,128)(2,1)} %all-gather.5.cloned.1.call-done) | copy-start | bytes 6291460
  138.9 25.9 %copy-start.9 = (f32[16,512]{1,0:T(8,128)S(1)}, f32[16,512]{1,0:T(8,128)}, u32[]{:S(2)}) copy-start(f32[16,512]{1,0:T(8,128)} %param.12) | copy-start | bytes 98308
  162.7 2.2 %copy-start.3 = (f32[16,64,512]{2,1,0:T(8,128)S(1)}, f32[16,64,512]{2,1,0:T(8,128)}, u32[]{:S(2)}) copy-start(f32[16,64,512]{2,1,0:T(8,128)} %fusion.22) | copy-start | bytes 6291460
  162.7 2.2 %copy-start.4 = (f32[512,512]{1,0:T(8,128)S(1)}, f32[512,512]{1,0:T(8,128)}, u32[]{:S(2)}) copy-start(f32[512,512]{1,0:T(8,128)} %fusion.33) | copy-start | bytes 3145732
  185.4 9.0 %copy-start.2 = (f32[512,1024]{1,0:T(8,128)S(1)}, f32[512,1024]{1,0:T(8,128)}, u32[]{:S(2)}) copy-start(f32[512,1024]{1,0:T(8,128)} %fusion.32) | copy-start | bytes 6291460
  185.4 9.0 %copy-start.7 = (f32[1024]{0:T(1024)S(1)}, f32[1024]{0:T(1024)}, u32[]{:S(2)}) copy-start(f32[1024]{0:T(1024)} %param.16) | copy-start | bytes 12292
  189.6 10.3 %all-to-all-start = ((f32[4,1,66]{2,1,0:T(1,128)}), f32[4,1,66]{2,1,0:T(1,128)S(1)}, u32[]{:S(2)}, u32[]{:S(2)}) async-start(f32[4,1,66]{2,1,0:T(1,128)} %bitcast.17), calls=%async_computation | async-start | bytes 4096 | tf_op jit(solution)/shard_map/all_to_all | solution.py:150
Sparse Core Ops, SparseCore 0:
  9.6 48.3 all-gather.4
  65.6 58.3 all-gather.6
where the time goes:
time: 208 us
  waiting for transfers between devices  51.4 us (25%)
  matrix products  50 us (24%)
  blocking collectives  40.1 us (19%)
  local copies, waits for them, and re-layouts  34.5 us (17%)
  between operations  14.9 us (7%)
  other arithmetic  12 us (6%)
  starting transfers between devices  4.76 us (2%)
    all_gather x1, waiting for transfers between devices, shards(): gathered = lax.all_gather(grad_out, 'exp', axis=0, tiled=True)  46 us
    unnamed x1, blocking collectives  23.5 us
    dot_general x1, matrix products, block_pass(): jnp.einsum('hut,thp->uhp', weights * intersection[None], grad_block, prec...  20.5 us
    convert_element_type x2, local copies, waits for them, and re-layouts, shards(): partial_scores = jnp.sum(projected * saved_rows.astype(jnp.float32), axis=1)  18.1 us
    all_gather x1, blocking collectives, shards(): lax.all_gather(summary[None], 'seq', axis=0, tiled=True)  16.7 us
    dot_general x1, matrix products, shards(): lax.dot_general(lax.all_gather(slot_rows, 'seq', axis=0, tiled=True), wei...  14.9 us
    gather x1, local copies, waits for them, and re-layouts, shards(): slot_rows = jnp.take(gathered, flat_index, axis=0)  6.22 us
    dot_general x1, matrix products, shards(): lax.dot_general(gathered, out_proj, (((1,), (1,)), ((), ())), preferred_e...  5.91 us
  transfers between devices with their start and end apart: 3, of which 3 were waited for; matrix products, arithmetic and copies ran while one was open for 22% of the time, Pallas kernels for 0%

commit v1 on v0

--- a/solution.py
+++ b/solution.py
@@ -2,6 +2,7 @@
 import jax.numpy as jnp
 from jax import lax
 from jax.sharding import PartitionSpec as P
+from jax.lax import axis_index, axis_size, ppermute
 
 HEAD = 64
 highest = lax.Precision.HIGHEST
@@ -91,7 +92,26 @@
     seq_count = lax.axis_size("seq")
     tok_len = grad_out.shape[0]
     cap_len = hidden_act.shape[2]
-    gathered = lax.all_gather(grad_out, "exp", axis=0, tiled=True)
+
+    def face_derive(x_in, peer_axis="exp"):
+        n_axis = axis_size(peer_axis)
+        series = []
+        ix = 1
+        while ix < n_axis:
+            series.append((ix - 1, ix))
+            ix = ix + 1
+        vec_out = series + [(n_axis - 1, 0)]
+        out_arr = x_in
+        windows = [out_arr]
+        q = 0
+        while q < n_axis - 1:
+            out_arr = ppermute(out_arr, axis_name=peer_axis, perm=vec_out)
+            windows += [out_arr]
+            q += 1
+        outcome_arr = jnp.concatenate([*reversed(windows)], axis=0)
+        return jnp.roll(outcome_arr, shift=(axis_index(peer_axis) + 1) * out_arr.shape[0], axis=0)
+
+    gathered = face_derive(grad_out)
     groups = expert_ids.reshape(exp_count, tok_len, expert_ids.shape[1])
     position, filled = route_table(groups, exp_index, cap_len)
     flat_index = (position + lax.broadcasted_iota(jnp.int32, position.shape, 0) * tok_len).reshape(

time: 208 us -> 202 us (0.971)
  waiting for transfers between devices: 51.4 us -> 43.3 us
  starting transfers between devices: 4.76 us -> 7.74 us
    all_gather x1 -> x0, waiting for transfers between devices: 46 us -> none  [shards(): gathered = lax.all_gather(grad_out, 'exp', axis=0, tiled=True)]
    ppermute x0 -> x3, waiting for transfers between devices: none -> 39.1 us  [face_derive(): out_arr = ppermute(out_arr, axis_name=peer_axis, perm=vec_out)]
    gather x1, local copies, waits for them, and re-layouts: 6.22 us -> 2.6 us  [shards(): slot_rows = jnp.take(gathered, flat_index, axis=0)]
    ppermute x0 -> x3, starting transfers between devices: none -> 3.11 us  [face_derive(): out_arr = ppermute(out_arr, axis_name=peer_axis, perm=vec_out)]
  transfers between devices with their start and end apart: 3 -> 5, of which waited for: 3 -> 5; matrix products, arithmetic and copies ran while one was open for 22% -> 23% of each run, Pallas kernels for 0% -> 0%
where the time goes in v1:
time: 202 us; the launch traced here: 201 us
  matrix products  51.1 us (25%)
  waiting for transfers between devices  43.3 us (21%)
  blocking collectives  39.7 us (20%)
  local copies, waits for them, and re-layouts  32.5 us (16%)
  between operations  14.9 us (7%)
  other arithmetic  12 us (6%)
  starting transfers between devices  7.74 us (4%)
    ppermute x3, waiting for transfers between devices, face_derive(): out_arr = ppermute(out_arr, axis_name=peer_axis, perm=vec_out)  39.1 us
    unnamed x1, blocking collectives  23.5 us
    dot_general x1, matrix products, block_pass(): jnp.einsum('hut,thp->uhp', weights * intersection[None], grad_block, prec...  21.6 us
    convert_element_type x2, local copies, waits for them, and re-layouts, shards(): partial_scores = jnp.sum(projected * saved_rows.astype(jnp.float32), axis=1)  18.5 us
    all_gather x1, blocking collectives, shards(): lax.all_gather(summary[None], 'seq', axis=0, tiled=True)  16.2 us
    dot_general x1, matrix products, shards(): lax.dot_general(lax.all_gather(slot_rows, 'seq', axis=0, tiled=True), wei...  14.9 us
    dot_general x1, matrix products, shards(): lax.dot_general(gathered, out_proj, (((1,), (1,)), ((), ())), preferred_e...  5.9 us
    all_to_all x1, starting transfers between devices, shards(): lax.all_to_all(summed.reshape(exp_count, 1, cap_len), 'exp', split_axis=0...  4.6 us
  transfers between devices with their start and end apart: 5, of which 5 were waited for; matrix products, arithmetic and copies ran while one was open for 23% of the time, Pallas kernels for 0%

profile of v1, /device:TPU:0, one launch (start us, length us, event | category | flops | bytes accessed | tf_op | source)
XLA Modules:
  0.0 201.2 jit_solution(15751425900371117789)
XLA Ops:
  7.2 3.1 %collective-permute-start = (bf16[128,2048]{1,0:T(8,128)(2,1)}, bf16[128,2048]{1,0:T(8,128)(2,1)S(1)}, u32[]{:S(2)}, u32[]{:S(2)}) collective-permute-start(bf16[128,2048]{1,0:T(8,128)(2,1)} %param.10), channel_id=1, source_target_pairs={{0,1},{1,2},{2,3},{3,0},{4,5},{5,6},{6,7},{7,4},{8,9},{9,10},{10,1... | collective-permute-start | bytes 1572872 | tf_op jit(solution)/shard_map/ppermute | solution.py:108
  10.3 0.7 compare_reduce_fusion
  11.4 13.1 %collective-permute-done = bf16[128,2048]{1,0:T(8,128)(2,1)S(1)} collective-permute-done((bf16[128,2048]{1,0:T(8,128)(2,1)}, bf16[128,2048]{1,0:T(8,128)(2,1)S(1)}, u32[]{:S(2)}, u32[]{:S(2)}) %collective-permute-start) | collective-permute-done | bytes 524320 | tf_op jit(solution)/shard_map/ppermute | solution.py:108
  24.5 1.2 select_reduce_fusion.1
  26.0 13.4 %collective-permute-done.1 = bf16[128,2048]{1,0:T(8,128)(2,1)S(1)} collective-permute-done((bf16[128,2048]{1,0:T(8,128)(2,1)S(1)}, bf16[128,2048]{1,0:T(8,128)(2,1)S(1)}, u32[]{:S(2)}, u32[]{:S(2)}) %collective-permute-start.1) | collective-permute-done | bytes 524320 | tf_op jit(solution)/shard_map/ppermute | solution.py:108
  39.4 1.2 fusion.21
  40.8 12.6 %collective-permute-done.2 = bf16[128,2048]{1,0:T(8,128)(2,1)S(1)} collective-permute-done((bf16[128,2048]{1,0:T(8,128)(2,1)S(1)}, bf16[128,2048]{1,0:T(8,128)(2,1)S(1)}, u32[]{:S(2)}, u32[]{:S(2)}) %collective-permute-start.2) | collective-permute-done | bytes 524320 | tf_op jit(solution)/shard_map/ppermute | solution.py:108
  53.5 1.1 constant_dynamic-update-slice_fusion.4
  55.0 2.6 %gather_fusion = bf16[264,2048]{1,0:T(8,128)(2,1)S(1)} fusion(bf16[512,2048]{1,0:T(8,128)(2,1)S(1)} %constant_dynamic-slice_fusion.2, s32[1024]{0:T(1024)S(1)} %pad_clamp_fusion), kind=kCustom, calls=%fused_computation | custom fusion | bytes 2163744 | tf_op jit(solution)/shard_map/jit(_take)/gather | solution.py:120
  57.6 1.2 select_select_fusion
  59.2 1.1 reduce-window.14
  60.5 1.2 reduce-window.16
  62.3 9.0 %copy.85 = f32[1,32,66,1024]{3,2,1,0:T(8,128)} copy(bf16[1,32,66,1024]{3,1,2,0:T(8,128)(2,1)} %param.18) | data formatting | bytes 12976128 | tf_op jit(solution)/shard_map/convert_element_type | solution.py:130
  71.3 9.5 %reshape.166 = f32[2112,1024]{1,0:T(8,128)} reshape(f32[1,32,66,1024]{3,2,1,0:T(8,128)} %copy.85) | data formatting | bytes 17301504 | tf_op jit(solution)/shard_map/convert_element_type | solution.py:130
  80.8 0.7 constant_dynamic-slice_fusion.1
  81.9 0.6 fusion.31
  83.9 2.0 fusion.33
  85.9 3.1 %fusion.22 = f32[16,64,512]{2,1,0:T(8,128)} fusion(f32[16,512]{1,0:T(8,128)S(1)} %copy-done), kind=kOutput, calls=%fused_computation.34 | convolution fusion | flops 100663296 | bytes 2129920 | tf_op jit(solution)/shard_map/while/body/eval_jaxpr/nu,hnp->uhp/dot_general | solution.py:29
  89.0 5.9 %fusion.32 = f32[512,1024]{1,0:T(8,128)} fusion(bf16[512,2048]{1,0:T(8,128)(2,1)S(1)} %constant_dynamic-slice_fusion.2, bf16[1024,2048]{1,0:T(8,128)(2,1)} %param.11), kind=kOutput, calls=%fused_computation.83 | convolution fusion | flops 2147483648 | bytes 8388608 | tf_op jit(solution)/shard_map/dot_general | solution.py:132
  94.9 1.9 copy.75
  96.8 1.8 convolution_add_fusion
  98.5 16.2 %all-gather.1 = f32[128,16,64]{2,1,0:T(8,128)S(1)} all-gather(f32[16,16,64]{2,1,0:T(8,128)S(1)} %convolution_add_fusion), channel_id=3, replica_groups=mesh['seq'=8,'exp'=4] {'seq'}, dimensions={0}, use_global_device_ids=true | all-gather | bytes 589824 | tf_op jit(solution)/shard_map/all_gather | solution.py:147
  114.8 1.7 all-gather.4.cloned.1.call-done
  116.5 14.9 %multiply_reduce_fusion = f32[2112]{0:T(1024)S(1)} fusion(f32[2112,1024]{1,0:T(8,128)} %reshape.166, bf16[2112,2048]{1,0:T(8,128)(2,1)} %all-gather.4.cloned.1.call-done, bf16[1,1024,2048]{2,1,0:T(8,128)(2,1)} %param.19), kind=kOutput, calls=%fused_computation.8 | convolution fusion | flops 8862693376 | bytes 21504256 | tf_op jit(solution)/shard_map/dot_general | solution.py:124
  131.5 23.5 %all-reduce.2 = (f32[128]{0:T(128)S(1)}, f32[8,4,66]{2,1,0:T(4,128)S(1)}) all-reduce(f32[128]{0:T(128)S(1)} %dynamic-update-slice, f32[8,4,66]{2,1,0:T(4,128)S(1)} %reshape.164), channel_id=2, replica_groups=mesh['seq'=8,'exp'=4] {'seq'}, use_global_device_ids=true, to_apply=%add | all-reduce | flops 2240 | bytes 17920
  155.5 1.8 fusion.24
  157.3 21.6 %fusion.12 = f32[512,16,64]{0,2,1:T(8,128)} fusion(f32[16,64,512]{2,1,0:T(8,128)S(1)} %fusion.24, f32[16,64,512]{2,1,0:T(8,128)} %fusion.22, f32[512,16,64]{0,2,1:T(8,128)S(1)} %bitcast.79, f32[512,512]{1,0:T(8,128)} %fusion.33, f32[16,512]{1,0:T(8,128)S(1)} %copy_bitcast_fusion.1, f32[512,16]{0,1:T(8,128)S(1)} %get-tuple-element.22, ...), kind=kOutput, calls=%fused_computation.16 | convolution fusion | flops 3244818432 | bytes 9568256 | tf_op jit(solution)/shard_map/while/body/eval_jaxpr/hut,thp->uhp/dot_general | solution.py:26
  178.9 3.1 %copy.80 = f32[512,1024]{1,0:T(8,128)} copy(f32[512,1024]{0,1:T(8,128)} %bitcast.81) | data formatting | bytes 4194304 | tf_op jit(solution)/shard_map/reshape | solution.py:163
  182.0 1.2 constant_dynamic-slice_fusion
  183.2 4.6 %all-to-all-start = ((f32[4,1,66]{2,1,0:T(1,128)}), f32[4,1,66]{2,1,0:T(1,128)S(1)}, u32[]{:S(2)}, u32[]{:S(2)}) async-start(f32[4,1,66]{2,1,0:T(1,128)} %bitcast.17), calls=%async_computation | async-start | bytes 4096 | tf_op jit(solution)/shard_map/all_to_all | solution.py:170
  187.8 3.1 %add_convert_fusion = bf16[512,1024]{1,0:T(8,128)(2,1)} fusion(f32[512,1024]{1,0:T(8,128)} %copy.80, f32[512,1024]{1,0:T(8,128)S(1)} %copy-done.1, f32[1024]{0:T(1024)S(1)} %copy-done.5), kind=kLoop, calls=%fused_computation.19 | loop fusion | flops 1572864 | bytes 5246976 | tf_op jit(solution)/shard_map/convert_element_type | solution.py:163
  190.9 2.5 %all-to-all-done = f32[4,1,66]{2,1,0:T(1,128)S(1)} async-done(((f32[4,1,66]{2,1,0:T(1,128)}), f32[4,1,66]{2,1,0:T(1,128)S(1)}, u32[]{:S(2)}, u32[]{:S(2)}) %all-to-all-start) | async-done | bytes 1088 | tf_op jit(solution)/shard_map/all_to_all | solution.py:170
  (76 shorter events, 5.1 us)
Async XLA Ops:
  7.2 76.7 %copy-start = (f32[16,512]{1,0:T(8,128)S(1)}, f32[16,512]{1,0:T(8,128)}, u32[]{:S(2)}) copy-start(f32[16,512]{1,0:T(8,128)} %param.14) | copy-start | bytes 98308
  7.2 47.6 %copy-start.2 = (bf16[128,2048]{1,0:T(8,128)(2,1)S(1)}, bf16[128,2048]{1,0:T(8,128)(2,1)}, u32[]{:S(2)}) copy-start(bf16[128,2048]{1,0:T(8,128)(2,1)} %param.10) | copy-start | bytes 1572868
  7.2 109.3 %all-gather.4.cloned.1.call-start = ((), (), s32[]{:S(2)}) async-start(), calls=%async_computation.1 | async-start | bytes 9732096 | tf_op jit(solution)/shard_map/all_gather | solution.py:125
  7.2 17.3 %collective-permute-start = (bf16[128,2048]{1,0:T(8,128)(2,1)}, bf16[128,2048]{1,0:T(8,128)(2,1)S(1)}, u32[]{:S(2)}, u32[]{:S(2)}) collective-permute-start(bf16[128,2048]{1,0:T(8,128)(2,1)} %param.10), channel_id=1, source_target_pairs={{0,1},{1,2},{2,3},{3,0},{4,5},{5,6},{6,7},{7,4},{8,9},{9,10},{10,1... | collective-permute-start | bytes 1572872 | tf_op jit(solution)/shard_map/ppermute | solution.py:108
  24.5 14.9 %collective-permute-start.1 = (bf16[128,2048]{1,0:T(8,128)(2,1)S(1)}, bf16[128,2048]{1,0:T(8,128)(2,1)S(1)}, u32[]{:S(2)}, u32[]{:S(2)}) collective-permute-start(bf16[128,2048]{1,0:T(8,128)(2,1)S(1)} %collective-permute-done), channel_id=1, source_target_pairs={{0,1},{1,2},{2,3},{3,0},{4,5},{5,6},{6,7},{7,4},{8,9},{9,10},{10,1... | collective-permute-start | bytes 1572872 | tf_op jit(solution)/shard_map/ppermute | solution.py:108
  39.4 14.0 %collective-permute-start.2 = (bf16[128,2048]{1,0:T(8,128)(2,1)S(1)}, bf16[128,2048]{1,0:T(8,128)(2,1)S(1)}, u32[]{:S(2)}, u32[]{:S(2)}) collective-permute-start(bf16[128,2048]{1,0:T(8,128)(2,1)S(1)} %collective-permute-done.1), channel_id=1, source_target_pairs={{0,1},{1,2},{2,3},{3,0},{4,5},{5,6},{6,7},{7,4},{8,9},{9,10},{10,1... | collective-permute-start | bytes 1572872 | tf_op jit(solution)/shard_map/ppermute | solution.py:108
  55.0 3.9 %copy-start.3 = (f32[16,512]{1,0:T(8,128)S(1)}, f32[16,512]{1,0:T(8,128)}, u32[]{:S(2)}) copy-start(f32[16,512]{1,0:T(8,128)} %param.13) | copy-start | bytes 98308
  71.3 10.6 %copy-start.6 = (u32[32]{0:T(128)S(1)}, u32[32]{0:T(128)}, u32[]{:S(2)}) copy-start(u32[32]{0:T(128)} %constant.97) | copy-start | bytes 388
  71.3 12.6 %copy-start.4 = (f32[16,512]{1,0:T(8,128)S(1)}, f32[16,512]{1,0:T(8,128)}, u32[]{:S(2)}) copy-start(f32[16,512]{1,0:T(8,128)} %param.15) | copy-start | bytes 98308
  114.8 42.5 %copy-start.7 = (f32[16,512]{1,0:T(8,128)S(1)}, f32[16,512]{1,0:T(8,128)}, u32[]{:S(2)}) copy-start(f32[16,512]{1,0:T(8,128)} %param.12) | copy-start | bytes 98308
  178.9 8.9 %copy-start.1 = (f32[512,1024]{1,0:T(8,128)S(1)}, f32[512,1024]{1,0:T(8,128)}, u32[]{:S(2)}) copy-start(f32[512,1024]{1,0:T(8,128)} %fusion.32) | copy-start | bytes 6291460
  178.9 8.9 %copy-start.5 = (f32[1024]{0:T(1024)S(1)}, f32[1024]{0:T(1024)}, u32[]{:S(2)}) copy-start(f32[1024]{0:T(1024)} %param.16) | copy-start | bytes 12292
  183.2 10.2 %all-to-all-start = ((f32[4,1,66]{2,1,0:T(1,128)}), f32[4,1,66]{2,1,0:T(1,128)S(1)}, u32[]{:S(2)}, u32[]{:S(2)}) async-start(f32[4,1,66]{2,1,0:T(1,128)} %bitcast.17), calls=%async_computation | async-start | bytes 4096 | tf_op jit(solution)/shard_map/all_to_all | solution.py:170
Sparse Core Ops, SparseCore 0:
  59.0 57.4 all-gather.3
